TPU v7x, 32 devices: a whole 2x2x4 slice. The times are simulated.
32 devices in a mesh: lat: 4 (over y, x), lon: 8 (over z, core).
Axes of the slice: x: 2, y: 2, z: 4, core: 2. Of those that a mesh axis runs over, the one named last changes fastest.
Arguments:
- latent_field: bfloat16 [640, 32, 64], P(None, 'lat', 'lon'), may hold values from -6 to 6
- spectral_filter: float32 [640, 32], P('lon'), may hold values from -5 to 5
- conv_weight: float32 [9, 640], replicated, may hold values from -2 to 2
- norm_gain: float32 [640], replicated, may hold values from 0.1 to 1.9
- weight_in: bfloat16 [640, 1280], replicated, may hold values from -0.25 to 0.25
- weight_out: bfloat16 [1280, 640], replicated, may hold values from -0.15625 to 0.15625
Outputs:
- updated: bfloat16 [640, 32, 64], P(None, 'lat', 'lon')
All inputs are finite; a program needn't handle non-finite values.
Results may differ from a plain program's by a relative error of at most 0.01.
Values may be sent and summed in bfloat16 or wider, within the bound.
A program may use at most 128 MiB of HBM per device.

v0:
```python
import functools
import math
import jax
import jax.numpy as jnp
import numpy as np
from jax import lax
from jax.sharding import PartitionSpec as P

highest = lax.Precision.HIGHEST
epsilon_norm = 1e-06


def with_halo(cells, sides, width):
    for axis, dim in sides:
        count = lax.axis_size(axis)
        ends = count - 1
        head = lax.slice_in_dim(cells, 0, width, axis=dim)
        tail = lax.slice_in_dim(cells, cells.shape[dim] - width, cells.shape[dim], axis=dim)
        cells = jnp.concatenate(
            [
                lax.ppermute(tail, axis, [(i, (i + 1) % count) for i in range(ends)]),
                cells,
                lax.ppermute(head, axis, [((i + 1) % count, i) for i in range(ends)]),
            ],
            axis=dim,
        )
    return cells


def quadrature(lat_count):
    colatitude = (jnp.arange(lat_count, dtype=jnp.float32) + 0.5) * (math.pi / lat_count)
    return jnp.sin(colatitude) * (math.pi / lat_count)


def fourier_tables(lon_count, mode_count):
    wave_index = (
        jnp.arange(mode_count, dtype=jnp.int32)[:, None]
        * jnp.arange(lon_count, dtype=jnp.int32)[None, :]
    )
    phase_angle = (wave_index % lon_count).astype(jnp.float32) * (2.0 * math.pi / lon_count)
    cosine = jnp.cos(phase_angle)
    sine_table = jnp.sin(phase_angle)
    angle_step = 2.0 * math.pi / lon_count
    forward = jnp.concatenate([angle_step * cosine, -angle_step * sine_table], axis=0)
    weight = jnp.where(jnp.arange(mode_count, dtype=jnp.int32) == 0, 1.0, 2.0).astype(jnp.float32)[
        :, None
    ]
    inverse = jnp.concatenate([weight * cosine, -weight * sine_table], axis=0)
    return (forward, inverse)


def legendre_rows(order_ids, lat_count):
    colatitude = (jnp.arange(lat_count, dtype=jnp.float32) + 0.5) * (math.pi / lat_count)
    cosine = jnp.cos(colatitude)
    sine_col = jnp.sin(colatitude)
    order_f = order_ids.astype(jnp.float32)
    factor_index = jnp.arange(1, lat_count, dtype=jnp.float32)
    ratio_log = jnp.log((2.0 * factor_index - 1.0) / (2.0 * factor_index))
    included = (factor_index[None, :] <= order_f[:, None]).astype(jnp.float32)
    log_factor = jnp.sum(included * ratio_log[None, :], axis=1)
    start_log = 0.5 * jnp.log((2.0 * order_f + 1.0) / (4.0 * math.pi)) + 0.5 * log_factor
    start_log = start_log[:, None] + order_f[:, None] * jnp.log(sine_col)[None, :]
    blank_rows = jnp.zeros((order_ids.shape[0], lat_count), jnp.float32)
    order_col = order_f[:, None]

    def advance(state_carry, degree):
        before, current, scale_log = state_carry
        degree_f = degree.astype(jnp.float32)
        alpha_term = jnp.sqrt(
            (4.0 * degree_f * degree_f - 1.0)
            / jnp.maximum(degree_f * degree_f - order_col * order_col, 1.0)
        )
        beta_term = jnp.sqrt(
            jnp.maximum((degree_f - 1.0) ** 2 - order_col * order_col, 0.0)
            / jnp.maximum(4.0 * (degree_f - 1.0) ** 2 - 1.0, 1.0)
        )
        stepped = alpha_term * (cosine[None, :] * current - beta_term * before)
        at_start = order_ids[:, None] == degree
        past_start = order_ids[:, None] < degree
        fresh_value = jnp.where(at_start, 1.0, jnp.where(past_start, stepped, 0.0))
        fresh_log = jnp.where(at_start, start_log, scale_log)
        entry_value = fresh_value * jnp.exp(fresh_log)
        rescale = jnp.where(
            past_start | at_start, jnp.maximum(jnp.abs(fresh_value), jnp.abs(current)), 1.0
        )
        return (
            (current / rescale, fresh_value / rescale, fresh_log + jnp.log(rescale)),
            entry_value,
        )

    degrees = jnp.arange(lat_count, dtype=jnp.int32)
    unused, legendre = lax.scan(advance, (blank_rows, blank_rows, blank_rows), degrees)
    return legendre


def filter_modes(banded, legendre, filter_block, quad_weights):
    coefficients = jnp.einsum(
        "lmj,pmcj->pmcl", legendre, banded * quad_weights[None, None, None, :], precision=highest
    )
    coefficients = coefficients * filter_block[None, None, :, :]
    return jnp.einsum("lmj,pmcl->pmcj", legendre, coefficients, precision=highest)


def wrap_columns(extended):
    return jnp.concatenate([extended[:, :, -1:], extended, extended[:, :, :1]], axis=2)


def depthwise_core(extended, kernel, lat_rows, lon_cols):
    accumulated = jnp.zeros((extended.shape[0], lat_rows, lon_cols), jnp.float32)
    for row_shift in range(3):
        for col_shift in range(3):
            piece = extended[
                :, row_shift : row_shift + lat_rows, col_shift : col_shift + lon_cols
            ].astype(jnp.float32)
            accumulated = accumulated + kernel[3 * row_shift + col_shift][:, None, None] * piece
    return accumulated.astype(jnp.bfloat16)


def channel_mlp(summed_low, norm_gain, weight_in, weight_out):
    summed = summed_low.astype(jnp.float32)
    scale_inv = lax.rsqrt(jnp.mean(summed * summed, axis=0, keepdims=True) + epsilon_norm)
    normed = (summed * scale_inv * norm_gain[:, None]).astype(jnp.bfloat16)
    hidden = lax.dot_general(
        weight_in, normed, (((0,), (0,)), ((), ())), preferred_element_type=jnp.float32
    )
    hidden = jax.nn.gelu(hidden, approximate=False).astype(jnp.bfloat16)
    result = summed + lax.dot_general(
        weight_out, hidden, (((0,), (0,)), ((), ())), preferred_element_type=jnp.float32
    )
    return result.astype(jnp.bfloat16)


def add_three(first, second, third):
    total = first.astype(jnp.float32) + second.astype(jnp.float32) + third.astype(jnp.float32)
    return total.astype(jnp.bfloat16)


def on_device(latent_field, spectral_filter, conv_weight, norm_gain, weight_in, weight_out):
    channels, lat_rows, lon_cols = latent_field.shape
    sector_count = lax.axis_size("lon")
    lat_count = lat_rows * lax.axis_size("lat")
    lon_count = lon_cols * sector_count
    chan_block = channels // sector_count
    spread = lax.all_to_all(latent_field, "lon", split_axis=0, concat_axis=2, tiled=True)
    forward, inverse = fourier_tables(lon_count, lat_count)
    flattened = spread.astype(jnp.float32).reshape(chan_block * lat_rows, lon_count)
    spectrum = lax.dot_general(forward, flattened, (((1,), (1,)), ((), ())), precision=highest)
    spectrum = spectrum.reshape(2, lat_count, chan_block, lat_rows)
    banded = lax.all_to_all(spectrum, "lat", split_axis=1, concat_axis=3, tiled=True)
    order_ids = lax.axis_index("lat") * lat_rows + jnp.arange(lat_rows, dtype=jnp.int32)
    legendre = legendre_rows(order_ids, lat_count)
    synthesized = filter_modes(banded, legendre, spectral_filter, quadrature(lat_count))
    regathered = lax.all_to_all(synthesized, "lat", split_axis=3, concat_axis=1, tiled=True)
    regridded = lax.dot_general(
        regathered.reshape(2 * lat_count, chan_block * lat_rows),
        inverse,
        (((0,), (0,)), ((), ())),
        precision=highest,
    )
    spectral = regridded.reshape(chan_block, lat_rows, lon_count).astype(jnp.bfloat16)
    own_kernel = lax.dynamic_slice_in_dim(
        conv_weight, lax.axis_index("lon") * chan_block, chan_block, 1
    )
    rimmed = with_halo(spread, (("lat", 1),), 1)
    sector_mix = depthwise_core(wrap_columns(rimmed), own_kernel, lat_rows, lon_count)
    sector_sum = add_three(spread, spectral, sector_mix)
    summed = lax.all_to_all(sector_sum, "lon", split_axis=2, concat_axis=0, tiled=True)
    summed = summed.reshape(channels, lat_rows * lon_cols)
    result = channel_mlp(summed, norm_gain, weight_in, weight_out)
    return result.reshape(channels, lat_rows, lon_cols)


def transform_factors(lat_count, lon_count):
    theta = (np.arange(lat_count) + 0.5) * (math.pi / lat_count)
    x, s = (np.cos(theta), np.sin(theta))
    quad = s * (math.pi / lat_count)
    phi = 2.0 * math.pi * np.arange(lon_count) / lon_count
    legendre, cosine, sine, degree, order = ([], [], [], [], [])
    for m in range(lat_count):
        k = np.arange(1, m + 1)
        log_start = 0.5 * (
            np.log((2 * m + 1) / (4 * math.pi)) + np.sum(np.log((2 * k - 1) / (2 * k)))
        )
        before, current = (np.zeros(lat_count), np.exp(log_start + m * np.log(s)))
        for l in range(m, lat_count):
            if l > m:
                a = math.sqrt((4.0 * l * l - 1) / (l * l - m * m))
                b = math.sqrt(((l - 1.0) ** 2 - m * m) / (4.0 * (l - 1) ** 2 - 1))
                before, current = (current, a * (x * current - b * before))
            legendre.append(current)
            cosine.append(np.cos(m * phi))
            sine.append(-np.sin(m * phi))
            degree.append(l)
            order.append(m)
    legendre = np.stack(legendre, 1)
    cosine, sine = (np.stack(cosine, 1), np.stack(sine, 1))
    degree, order = (np.array(degree), np.array(order))
    legendre = np.concatenate([legendre, legendre], 1)
    fourier = np.concatenate([cosine, sine], 1)
    weight = np.where(np.concatenate([order, order]) == 0, 1.0, 2.0)
    select = np.arange(lat_count)[:, None] == np.concatenate([degree, degree])[None, :]
    forward = fourier * (2.0 * math.pi / lon_count)
    f32 = np.float32
    return (
        (legendre * quad[:, None]).astype(f32),
        forward.astype(f32),
        legendre.astype(f32),
        (fourier * weight).astype(f32),
        select.astype(f32),
    )


def full_table(rows, columns, lat_devices, lon_devices):
    width = rows.shape[1]
    rows = jnp.asarray(rows).reshape(lat_devices, 1, -1, 1, width)
    columns = jnp.asarray(columns).reshape(1, lon_devices, 1, -1, width)
    return (rows * columns).astype(jnp.bfloat16).reshape(-1, width)


def whole_sphere(
    lat_devices,
    lon_devices,
    latent_field,
    spectral_filter,
    conv_weight,
    norm_gain,
    weight_in,
    weight_out,
):
    channels, lat_rows, lon_cols = latent_field.shape
    devices = lat_devices * lon_devices
    lat_count, lon_count = (lat_rows * lat_devices, lon_cols * lon_devices)
    points = lat_rows * lon_cols
    own = channels // devices
    me_lat, me_lon = (lax.axis_index("lat"), lax.axis_index("lon"))
    start = (me_lat * lon_devices + me_lon) * own
    axes = ("lat", "lon")
    mine = lax.all_to_all(
        latent_field.reshape(devices, own, points), axes, split_axis=0, concat_axis=0, tiled=True
    )
    rows_f, cols_f, rows_i, cols_i, select = transform_factors(lat_count, lon_count)
    analysis = full_table(rows_f, cols_f, lat_devices, lon_devices)
    synthesis = full_table(rows_i, cols_i, lat_devices, lon_devices)
    filters = lax.all_gather(spectral_filter, "lon", axis=0, tiled=True)
    own_filter = lax.dynamic_slice_in_dim(filters, start, own, 0)
    gain = lax.dot_general(
        own_filter, jnp.asarray(select), (((1,), (0,)), ((), ())), precision=highest
    )
    flat = jnp.transpose(mine, (1, 0, 2)).reshape(own, devices * points)
    coefficients = lax.dot_general(
        flat, analysis, (((1,), (0,)), ((), ())), preferred_element_type=jnp.float32
    )
    coefficients = (coefficients * gain).astype(jnp.bfloat16)
    spectral = lax.dot_general(
        coefficients, synthesis, (((1,), (1,)), ((), ())), preferred_element_type=jnp.float32
    ).astype(jnp.bfloat16)
    spectral = spectral.reshape(own, lat_devices, lon_devices, lat_rows, lon_cols)
    own_kernel = lax.dynamic_slice_in_dim(conv_weight, start, own, 1)
    grid = flat.reshape(own, lat_devices, lon_devices, lat_rows, lon_cols)
    grid = jnp.transpose(grid, (0, 1, 3, 2, 4)).reshape(own, lat_count, lon_count)
    spectral = jnp.transpose(spectral, (0, 1, 3, 2, 4)).reshape(own, lat_count, lon_count)
    rimmed = jnp.pad(grid, ((0, 0), (1, 1), (0, 0)))
    mix = depthwise_core(wrap_columns(rimmed), own_kernel, lat_count, lon_count)
    total = add_three(grid, spectral, mix)
    total = total.reshape(own, lat_devices, lat_rows, lon_devices, lon_cols)
    total = jnp.transpose(total, (1, 3, 0, 2, 4)).reshape(devices, own, points)
    summed = lax.all_to_all(total, axes, split_axis=0, concat_axis=0, tiled=True)
    result = channel_mlp(summed.reshape(channels, points), norm_gain, weight_in, weight_out)
    return result.reshape(channels, lat_rows, lon_cols)


def whole_or_banded(lat_devices, lon_devices, *arguments):
    if arguments[0].shape[0] % (lat_devices * lon_devices) == 0:
        return whole_sphere(lat_devices, lon_devices, *arguments)
    return on_device(*arguments)


def solution(mesh):
    return jax.shard_map(
        functools.partial(whole_or_banded, mesh.shape["lat"], mesh.shape["lon"]),
        mesh=mesh,
        in_specs=(P(None, "lat", "lon"), P("lon", None), P(), P(), P(), P()),
        out_specs=P(None, "lat", "lon"),
        check_vma=False,
    )
```

profile of v0, /device:TPU:0, one launch (start us, length us, event | category | flops | bytes accessed | tf_op | source)
XLA Modules:
  0.0 63.5 jit_solution(10295145786277437358)
XLA Ops:
  0.0 0.0 copy-start
  0.0 0.0 copy-start.3
  0.0 0.0 copy-start.2
  0.0 2.3 %reshape.71 = bf16[32,20,64]{1,0,2:T(8,128)(2,1)S(1)} reshape(bf16[640,8,8]{0,2,1:T(8,128)(2,1)} %param.11) | data formatting | bytes 163840 | tf_op jit(solution)/shard_map/reshape | solution.py:239
  2.3 0.7 %copy.75 = bf16[32,20,64]{2,1,0:T(8,128)(2,1)S(1)} copy(bf16[32,20,64]{1,0,2:T(8,128)(2,1)S(1)} %reshape.71) | data formatting | bytes 163840 | tf_op jit(solution)/shard_map/reshape | solution.py:239
  3.0 0.8 %reshape.82 = bf16[32,2,640]{2,1,0:T(2,128)(2,1)} reshape(bf16[32,20,64]{2,1,0:T(8,128)(2,1)S(1)} %copy.75) | data formatting | bytes 163840
  3.8 7.3 %all-to-all-start = ((bf16[32,2,640]{2,1,0:T(2,128)(2,1)}), bf16[32,2,640]{2,1,0:T(2,128)(2,1)S(1)}, u32[]{:S(2)}, u32[]{:S(2)}) async-start(bf16[32,2,640]{2,1,0:T(2,128)(2,1)} %reshape.82), calls=%async_computation | async-start | bytes 163840 | tf_op jit(solution)/shard_map/all_to_all | solution.py:238
  11.1 0.0 copy-start.5
  11.1 4.4 %multiply_convert_fusion.1 = bf16[4,8,8,8,1056]{4,3,2,1,0:T(8,128)(2,1)} fusion(f32[8,8,1056]{2,1,0:T(8,128)} %constant.102, f32[4,8,1056]{2,1,0:T(8,128)} %constant.101), kind=kLoop, calls=%fused_computation.1 | loop fusion | flops 4325376 | bytes 4730880 | tf_op jit(solution)/shard_map/convert_element_type | solution.py:217
  15.6 0.0 copy-done.3
  15.6 0.0 copy-done.2
  15.6 3.4 %multiply_convert_fusion = bf16[4,8,8,8,1056]{4,3,2,1,0:T(8,128)(2,1)} fusion(f32[8,8,1056]{2,1,0:T(8,128)S(1)} %copy-done.2, f32[4,8,1056]{2,1,0:T(8,128)S(1)} %copy-done.3), kind=kLoop, calls=%fused_computation | loop fusion | flops 4325376 | bytes 4730880 | tf_op jit(solution)/shard_map/convert_element_type | solution.py:217
  19.0 0.0 copy-start.4
  19.0 0.0 copy-done.5
  19.0 14.4 %all-gather = f32[8,80,32]{1,2,0:T(8,128)S(1)} all-gather(f32[1,80,32]{1,2,0:T(8,128)S(1)} %bitcast.133), channel_id=1, replica_groups=mesh['lat'=4,'lon'=8] {'lon'}, dimensions={0}, use_global_device_ids=true | all-gather | bytes 92160 | tf_op jit(solution)/shard_map/all_gather | solution.py:244
  33.4 0.1 copy.80
  33.5 0.1 reshape.81
  33.6 1.1 %dynamic-slice_bitcast_fusion.8 = (f32[20]{0:T(128)S(1)}, f32[20]{0:T(128)S(1)}, f32[20]{0:T(128)S(1)}, f32[20]{0:T(128)S(1)}, f32[20]{0:T(128)S(1)}, /*index=5*...) fusion(f32[9,640]{1,0:T(8,128)} %param.13, s32[]{:T(128)S(6)} %select_n.4, s32[]{:T(128)S(6)} %add.74, ...), kind=kLoop, calls=%fused_computation.103 | loop fusion | bytes 1476 | tf_op jit(solution)/shard_map/mul | solution.py:115
  34.6 0.0 all-to-all-done
  34.7 0.2 reshape.83
  34.8 0.3 copy.76
  35.2 0.2 reshape.73
  35.4 0.0 copy-start.1
  35.4 3.2 %convolution_bitcast_fusion = f32[20,1056]{1,0:T(8,128)S(1)} fusion(bf16[2048,1056]{1,0:T(8,128)(2,1)} %bitcast.124, bf16[20,2048]{1,0:T(8,128)(2,1)S(1)} %reshape.73), kind=kOutput, calls=%fused_computation.3 | convolution fusion | flops 86507520 | bytes 4491776 | tf_op jit(solution)/shard_map/dot_general | solution.py:250
  38.6 0.0 copy-done.4
  38.6 0.4 fusion
  39.0 0.1 copy-done.1
  39.1 1.3 %fusion.1 = f32[20,2048]{1,0:T(8,128)S(1)} fusion(bf16[20,1056]{1,0:T(8,128)(2,1)S(1)} %fusion, bf16[2048,1056]{1,0:T(8,128)(2,1)S(1)} %bitcast.125), kind=kOutput, calls=%fused_computation.6 | convolution fusion | flops 86589440 | bytes 4531456 | tf_op jit(solution)/shard_map/dot_general | solution.py:254
  40.4 0.4 copy.81
  40.8 1.1 %copy.82 = f32[20,4,8,8,8]{0,4,3,2,1:T(8,128)} copy(f32[20,4,8,8,8]{0,4,2,3,1:T(8,128)S(1)} %bitcast.126) | data formatting | bytes 327680 | tf_op jit(solution)/shard_map/convert_element_type | solution.py:134
  41.9 0.0 copy-start.6
  41.9 1.7 %copy.83 = f32[20,32,64]{2,1,0:T(8,128)S(1)} copy(f32[20,32,64]{0,2,1:T(8,128)} %bitcast.127) | data formatting | bytes 327680 | tf_op jit(solution)/shard_map/convert_element_type | solution.py:134
  43.6 0.1 copy.77
  43.8 0.4 copy.78
  44.1 0.2 pad_slice_fusion.9
  44.3 0.1 pad.4
  44.4 1.1 %fusion.6 = bf16[20,32,64]{2,1,0:T(8,128)(2,1)S(1)} fusion(f32[20,32,64]{2,1,0:T(8,128)S(1)} %copy.83, bf16[20,32,64]{2,1,0:T(8,128)(2,1)S(1)} %copy.78, bf16[20,34,64]{2,1,0:T(8,128)(2,1)S(1)} %pad.4, bf16[20,34,1]{2,1,0:T(8,128)(2,1)S(1)} %get-tuple-element.6, bf16[20,34,1]{2,1,0:T(8,128)(2,1)S(1)} %get-tuple-element.5, f32[20]{0:T(128)S(1)} %get-tuple-element.15, ...), kind=kLoop, calls=%fused_computation.16 | loop fusion | flops 2007040 | bytes 1520128 | tf_op jit(solution)/shard_map/convert_element_type | solution.py:135
  45.5 0.4 copy.85
  45.9 0.1 copy.86
  46.0 0.3 copy.87
  46.3 0.1 reshape.84
  46.5 12.9 %all_to_all.10 = bf16[32,2,640]{2,1,0:T(2,128)(2,1)S(1)} all-to-all(bf16[32,2,640]{2,1,0:T(2,128)(2,1)S(1)} %reshape.84), channel_id=1, replica_groups=mesh['lat'=4,'lon'=8] {'lat','lon'}, dimensions={0} | all-to-all | bytes 163840 | tf_op jit(solution)/shard_map/all_to_all | solution.py:267
  59.3 0.2 reshape.85
  59.6 0.1 multiply_reduce_fusion
  59.7 0.1 copy.88
  59.8 0.0 copy-done
  59.9 0.0 copy-done.6
  59.9 3.6 %fusion.4 = bf16[640,8,8]{0,2,1:T(8,128)(2,1)} fusion(f32[640,64]{0,1:T(8,128)S(1)} %copy.88, bf16[1280,640]{1,0:T(8,128)(2,1)S(1)} %copy-done, bf16[640,1280]{1,0:T(8,128)(2,1)} %param.15, f32[640,64]{1,0:T(8,128)S(1)} %reshape.78, f32[640]{0:T(1024)S(1)} %copy-done.6, f32[64]{0:T(128)S(1)} %add_rsqrt_fusion), kind=kOutput, calls=%fused_computation.10 | convolution fusion | flops 215244800 | bytes 3689216 | tf_op jit(solution)/shard_map/dot_general | solution.py:127
  (3 shorter events, 0.1 us)
Async XLA Ops:
  0.0 59.8 %copy-start = (bf16[1280,640]{1,0:T(8,128)(2,1)S(1)}, bf16[1280,640]{1,0:T(8,128)(2,1)}, u32[]{:S(2)}) copy-start(bf16[1280,640]{1,0:T(8,128)(2,1)} %param.16) | copy-start | bytes 4915204
  0.0 15.6 %copy-start.3 = (f32[4,8,1056]{2,1,0:T(8,128)S(1)}, f32[4,8,1056]{2,1,0:T(8,128)}, u32[]{:S(2)}) copy-start(f32[4,8,1056]{2,1,0:T(8,128)} %constant.103) | copy-start | bytes 405508
  0.0 15.6 %copy-start.2 = (f32[8,8,1056]{2,1,0:T(8,128)S(1)}, f32[8,8,1056]{2,1,0:T(8,128)}, u32[]{:S(2)}) copy-start(f32[8,8,1056]{2,1,0:T(8,128)} %constant.104) | copy-start | bytes 811012
  3.8 30.9 %all-to-all-start = ((bf16[32,2,640]{2,1,0:T(2,128)(2,1)}), bf16[32,2,640]{2,1,0:T(2,128)(2,1)S(1)}, u32[]{:S(2)}, u32[]{:S(2)}) async-start(bf16[32,2,640]{2,1,0:T(2,128)(2,1)} %reshape.82), calls=%async_computation | async-start | bytes 163840 | tf_op jit(solution)/shard_map/all_to_all | solution.py:238
  11.1 7.9 %copy-start.5 = (f32[80,32]{0,1:T(8,128)S(1)}, f32[80,32]{0,1:T(8,128)}, u32[]{:S(2)}) copy-start(f32[80,32]{0,1:T(8,128)} %param.12) | copy-start | bytes 30724
  19.0 19.6 %copy-start.4 = (f32[32,1056]{1,0:T(8,128)S(1)}, f32[32,1056]{1,0:T(8,128)}, u32[]{:S(2)}) copy-start(f32[32,1056]{1,0:T(8,128)} %constant.98.clone) | copy-start | bytes 405508
  35.4 3.8 %copy-start.1 = (bf16[4,8,8,8,1056]{4,3,2,1,0:T(8,128)(2,1)S(1)}, bf16[4,8,8,8,1056]{4,3,2,1,0:T(8,128)(2,1)}, u32[]{:S(2)}) copy-start(bf16[4,8,8,8,1056]{4,3,2,1,0:T(8,128)(2,1)} %multiply_convert_fusion) | copy-start | bytes 12976132
  41.9 17.9 %copy-start.6 = (f32[640]{0:T(1024)S(1)}, f32[640]{0:T(1024)}, u32[]{:S(2)}) copy-start(f32[640]{0:T(1024)} %param.14) | copy-start | bytes 7684
where the time goes:
time: 63.8 us; the launch traced here: 63.5 us
  blocking collectives  27.3 us (43%)
  local copies, waits for them, and re-layouts  11 us (17%)
  other arithmetic  9.14 us (14%)
  matrix products  8.54 us (13%)
  starting transfers between devices  7.33 us (11%)
    all_gather x1, blocking collectives, whole_sphere(): filters = lax.all_gather(spectral_filter, 'lon', axis=0, tiled=True)  14.4 us
    all_to_all x1, blocking collectives, whole_sphere(): lax.all_to_all(total, axes, split_axis=0, concat_axis=0, tiled=True)  12.9 us
    convert_element_type x2, other arithmetic, full_table(): return (rows * columns).astype(jnp.bfloat16).reshape(-1, width)  7.86 us
    all_to_all x1, starting transfers between devices, whole_sphere(): lax.all_to_all(latent_field.reshape(devices, own, points), axes, split_ax...  7.33 us
    dot_general x1, matrix products, channel_mlp(): lax.dot_general(weight_out, hidden, (((0,), (0,)), ((), ())), preferred_e...  3.62 us
    dot_general x1, matrix products, whole_sphere(): lax.dot_general(flat, analysis, (((1,), (0,)), ((), ())), preferred_eleme...  3.21 us
    convert_element_type x3, local copies, waits for them, and re-layouts, add_three(): second.astype(jnp.float32)  3.16 us
    reshape x2, local copies, waits for them, and re-layouts, whole_sphere(): latent_field.reshape(devices, own, points)  2.95 us
  transfers between devices with their start and end apart: 1, of which 0 were waited for; matrix products, arithmetic and copies ran while one was open for 14% of the time, Pallas kernels for 0%

commit v1 on v0

--- a/solution.py
+++ b/solution.py
@@ -241,7 +241,12 @@
     rows_f, cols_f, rows_i, cols_i, select = transform_factors(lat_count, lon_count)
     analysis = full_table(rows_f, cols_f, lat_devices, lon_devices)
     synthesis = full_table(rows_i, cols_i, lat_devices, lon_devices)
-    filters = lax.all_gather(spectral_filter, "lon", axis=0, tiled=True)
+    ring = [spectral_filter]
+    for hop in range(7):
+        ring.append(lax.ppermute(ring[-1], "lon", [(dev, (dev + 1) % 8) for dev in range(8)]))
+    filters = jnp.roll(
+        jnp.concatenate(ring[::-1], axis=0), (lax.axis_index("lon") + 1) * ring[0].shape[0], axis=0
+    )
     own_filter = lax.dynamic_slice_in_dim(filters, start, own, 0)
     gain = lax.dot_general(
         own_filter, jnp.asarray(select), (((1,), (0,)), ((), ())), precision=highest

time: 63.8 us -> 68.3 us (1.071)
  waiting for transfers between devices: 0.01 us -> 21.4 us
  blocking collectives: 27.3 us -> 10.1 us
    ppermute x0 -> x7, waiting for transfers between devices: none -> 21.4 us  [whole_sphere(): lax.ppermute(ring[-1], 'lon', [(dev, (dev + 1) % 8) for dev in range(8)])]
    all_gather x1 -> x0, blocking collectives: 14.4 us -> none  [whole_sphere(): filters = lax.all_gather(spectral_filter, 'lon', axis=0, tiled=True)]
    all_to_all x1, blocking collectives: 12.9 us -> 10.1 us  [whole_sphere(): lax.all_to_all(total, axes, split_axis=0, concat_axis=0, tiled=True)]
    ppermute x0 -> x7, starting transfers between devices: none -> 1.48 us  [whole_sphere(): lax.ppermute(ring[-1], 'lon', [(dev, (dev + 1) % 8) for dev in range(8)])]
    all_to_all x1, starting transfers between devices: 7.33 us -> 6.28 us  [whole_sphere(): lax.all_to_all(latent_field.reshape(devices, own, points), axes, split_ax...]
    unnamed x19 -> x18, local copies, waits for them, and re-layouts: 1.52 us -> 1.42 us
  transfers between devices with their start and end apart: 1 -> 8, of which waited for: 0 -> 6; matrix products, arithmetic and copies ran while one was open for 14% -> 19% of each run, Pallas kernels for 0% -> 0%
where the time goes in v1:
time: 68.3 us; the launch traced here: 68 us
  waiting for transfers between devices  21.4 us (31%)
  local copies, waits for them, and re-layouts  10.8 us (16%)
  blocking collectives  10.1 us (15%)
  other arithmetic  9.12 us (13%)
  matrix products  8.55 us (13%)
  starting transfers between devices  7.76 us (11%)
    ppermute x7, waiting for transfers between devices, whole_sphere(): lax.ppermute(ring[-1], 'lon', [(dev, (dev + 1) % 8) for dev in range(8)])  21.4 us
    all_to_all x1, blocking collectives, whole_sphere(): lax.all_to_all(total, axes, split_axis=0, concat_axis=0, tiled=True)  10.1 us
    convert_element_type x2, other arithmetic, full_table(): return (rows * columns).astype(jnp.bfloat16).reshape(-1, width)  7.85 us
    all_to_all x1, starting transfers between devices, whole_sphere(): lax.all_to_all(latent_field.reshape(devices, own, points), axes, split_ax...  6.28 us
    dot_general x1, matrix products, channel_mlp(): lax.dot_general(weight_out, hidden, (((0,), (0,)), ((), ())), preferred_e...  3.62 us
    dot_general x1, matrix products, whole_sphere(): lax.dot_general(flat, analysis, (((1,), (0,)), ((), ())), preferred_eleme...  3.21 us
    convert_element_type x3, local copies, waits for them, and re-layouts, add_three(): second.astype(jnp.float32)  3.17 us
    reshape x2, local copies, waits for them, and re-layouts, whole_sphere(): latent_field.reshape(devices, own, points)  2.81 us
  transfers between devices with their start and end apart: 8, of which 6 were waited for; matrix products, arithmetic and copies ran while one was open for 19% of the time, Pallas kernels for 0%

profile of v1, /device:TPU:0, one launch (start us, length us, event | category | flops | bytes accessed | tf_op | source)
XLA Modules:
  0.0 68.0 jit_solution(6061464414055936667)
XLA Ops:
  0.0 0.6 collective-permute-start
  0.6 5.7 %collective-permute-done = f32[80,32]{0,1:T(8,128)S(1)} collective-permute-done((f32[80,32]{0,1:T(8,128)}, f32[80,32]{0,1:T(8,128)S(1)}, u32[]{:S(2)}, u32[]{:S(2)}) %collective-permute-start) | collective-permute-done | bytes 10272 | tf_op jit(solution)/shard_map/ppermute | solution.py:246
  6.2 0.0 collective-permute-start.1
  6.2 5.0 %collective-permute-done.1 = f32[80,32]{0,1:T(8,128)S(1)} collective-permute-done((f32[80,32]{0,1:T(8,128)S(1)}, f32[80,32]{0,1:T(8,128)S(1)}, u32[]{:S(2)}, u32[]{:S(2)}) %collective-permute-start.1) | collective-permute-done | bytes 10272 | tf_op jit(solution)/shard_map/ppermute | solution.py:246
  11.2 0.0 collective-permute-start.2
  11.2 5.0 %collective-permute-done.2 = f32[80,32]{0,1:T(8,128)S(1)} collective-permute-done((f32[80,32]{0,1:T(8,128)S(1)}, f32[80,32]{0,1:T(8,128)S(1)}, u32[]{:S(2)}, u32[]{:S(2)}) %collective-permute-start.2) | collective-permute-done | bytes 10272 | tf_op jit(solution)/shard_map/ppermute | solution.py:246
  16.1 0.0 collective-permute-start.3
  16.1 2.1 %reshape.71 = bf16[32,20,64]{1,0,2:T(8,128)(2,1)S(1)} reshape(bf16[640,8,8]{0,2,1:T(8,128)(2,1)} %param.11) | data formatting | bytes 163840 | tf_op jit(solution)/shard_map/reshape | solution.py:239
  18.3 0.7 copy.70
  19.0 0.8 %reshape.80 = bf16[32,2,640]{2,1,0:T(2,128)(2,1)} reshape(bf16[32,20,64]{2,1,0:T(8,128)(2,1)S(1)} %copy.70) | data formatting | bytes 163840
  19.7 6.3 %all-to-all-start = ((bf16[32,2,640]{2,1,0:T(2,128)(2,1)}), bf16[32,2,640]{2,1,0:T(2,128)(2,1)S(1)}, u32[]{:S(2)}, u32[]{:S(2)}) async-start(bf16[32,2,640]{2,1,0:T(2,128)(2,1)} %reshape.80), calls=%async_computation | async-start | bytes 163840 | tf_op jit(solution)/shard_map/all_to_all | solution.py:238
  26.0 0.0 copy-start.5
  26.1 0.0 collective-permute-done.3
  26.1 0.3 collective-permute-start.4
  26.4 4.4 %multiply_convert_fusion.1 = bf16[4,8,8,8,1056]{4,3,2,1,0:T(8,128)(2,1)} fusion(f32[8,8,1056]{2,1,0:T(8,128)} %constant.133, f32[4,8,1056]{2,1,0:T(8,128)} %constant.132), kind=kLoop, calls=%fused_computation.1 | loop fusion | flops 4325376 | bytes 4730880 | tf_op jit(solution)/shard_map/convert_element_type | solution.py:217
  30.8 1.0 %collective-permute-done.4 = f32[80,32]{0,1:T(8,128)S(1)} collective-permute-done((f32[80,32]{0,1:T(8,128)S(1)}, f32[80,32]{0,1:T(8,128)S(1)}, u32[]{:S(2)}, u32[]{:S(2)}) %collective-permute-start.4) | collective-permute-done | bytes 10272 | tf_op jit(solution)/shard_map/ppermute | solution.py:246
  31.8 0.6 collective-permute-start.5
  32.4 3.4 %multiply_convert_fusion = bf16[4,8,8,8,1056]{4,3,2,1,0:T(8,128)(2,1)} fusion(f32[8,8,1056]{2,1,0:T(8,128)S(1)} %copy-done.2, f32[4,8,1056]{2,1,0:T(8,128)S(1)} %copy-done.3), kind=kLoop, calls=%fused_computation | loop fusion | flops 4325376 | bytes 4730880 | tf_op jit(solution)/shard_map/convert_element_type | solution.py:217
  35.9 0.9 %collective-permute-done.5 = f32[80,32]{0,1:T(8,128)S(1)} collective-permute-done((f32[80,32]{0,1:T(8,128)S(1)}, f32[80,32]{0,1:T(8,128)S(1)}, u32[]{:S(2)}, u32[]{:S(2)}) %collective-permute-start.5) | collective-permute-done | bytes 10272 | tf_op jit(solution)/shard_map/ppermute | solution.py:246
  36.8 1.1 %dynamic-slice_bitcast_fusion.8 = (f32[20]{0:T(128)S(1)}, f32[20]{0:T(128)S(1)}, f32[20]{0:T(128)S(1)}, f32[20]{0:T(128)S(1)}, f32[20]{0:T(128)S(1)}, /*index=5*...) fusion(f32[9,640]{1,0:T(8,128)} %param.13, s32[]{:T(128)S(6)} %select_n.21, s32[]{:T(128)S(6)} %add.92, ...), kind=kLoop, calls=%fused_computation.103 | loop fusion | bytes 1476 | tf_op jit(solution)/shard_map/mul | solution.py:115
  37.9 3.9 %collective-permute-done.6 = f32[80,32]{0,1:T(8,128)S(1)} collective-permute-done((f32[80,32]{0,1:T(8,128)S(1)}, f32[80,32]{0,1:T(8,128)S(1)}, u32[]{:S(2)}, u32[]{:S(2)}) %collective-permute-start.6) | collective-permute-done | bytes 10272 | tf_op jit(solution)/shard_map/ppermute | solution.py:246
  41.8 0.1 concatenate.17
  41.9 0.0 all-to-all-done
  41.9 0.2 reshape.81
  42.1 0.3 copy.71
  42.4 0.2 reshape.73
  42.6 3.2 %convolution_bitcast_fusion = f32[20,1056]{1,0:T(8,128)S(1)} fusion(bf16[2048,1056]{1,0:T(8,128)(2,1)} %bitcast.121, bf16[20,2048]{1,0:T(8,128)(2,1)S(1)} %reshape.73), kind=kOutput, calls=%fused_computation.3 | convolution fusion | flops 86507520 | bytes 4491776 | tf_op jit(solution)/shard_map/dot_general | solution.py:255
  45.8 0.0 copy-done.4
  45.8 0.4 fusion
  46.2 0.1 copy-done.1
  46.4 1.3 %fusion.1 = f32[20,2048]{1,0:T(8,128)S(1)} fusion(bf16[20,1056]{1,0:T(8,128)(2,1)S(1)} %fusion, bf16[2048,1056]{1,0:T(8,128)(2,1)S(1)} %bitcast.122), kind=kOutput, calls=%fused_computation.6 | convolution fusion | flops 86589440 | bytes 4531456 | tf_op jit(solution)/shard_map/dot_general | solution.py:259
  47.7 0.4 copy.75
  48.1 1.1 %copy.76 = f32[20,4,8,8,8]{0,4,3,2,1:T(8,128)} copy(f32[20,4,8,8,8]{0,4,2,3,1:T(8,128)S(1)} %bitcast.123) | data formatting | bytes 327680 | tf_op jit(solution)/shard_map/convert_element_type | solution.py:134
  49.2 1.7 %copy.77 = f32[20,32,64]{2,1,0:T(8,128)S(1)} copy(f32[20,32,64]{0,2,1:T(8,128)} %bitcast.124) | data formatting | bytes 327680 | tf_op jit(solution)/shard_map/convert_element_type | solution.py:134
  50.9 0.1 copy.72
  51.0 0.4 copy.73
  51.4 0.2 pad_slice_fusion.9
  51.6 0.1 pad.4
  51.6 1.1 %fusion.6 = bf16[20,32,64]{2,1,0:T(8,128)(2,1)S(1)} fusion(f32[20,32,64]{2,1,0:T(8,128)S(1)} %copy.77, bf16[20,32,64]{2,1,0:T(8,128)(2,1)S(1)} %copy.73, bf16[20,34,64]{2,1,0:T(8,128)(2,1)S(1)} %pad.4, bf16[20,34,1]{2,1,0:T(8,128)(2,1)S(1)} %get-tuple-element.6, bf16[20,34,1]{2,1,0:T(8,128)(2,1)S(1)} %get-tuple-element.5, f32[20]{0:T(128)S(1)} %get-tuple-element.15, ...), kind=kLoop, calls=%fused_computation.16 | loop fusion | flops 2007040 | bytes 1520128 | tf_op jit(solution)/shard_map/convert_element_type | solution.py:135
  52.8 0.4 copy.79
  53.1 0.1 copy.80
  53.3 0.3 copy.81
  53.6 0.1 reshape.82
  53.7 10.1 %all_to_all.10 = bf16[32,2,640]{2,1,0:T(2,128)(2,1)S(1)} all-to-all(bf16[32,2,640]{2,1,0:T(2,128)(2,1)S(1)} %reshape.82), channel_id=1, replica_groups=mesh['lat'=4,'lon'=8] {'lat','lon'}, dimensions={0} | all-to-all | bytes 163840 | tf_op jit(solution)/shard_map/all_to_all | solution.py:272
  63.9 0.2 reshape.83
  64.1 0.1 multiply_reduce_fusion
  64.2 0.1 copy.82
  64.4 3.6 %fusion.4 = bf16[640,8,8]{0,2,1:T(8,128)(2,1)} fusion(f32[640,64]{0,1:T(8,128)S(1)} %copy.82, bf16[1280,640]{1,0:T(8,128)(2,1)S(1)} %copy-done, bf16[640,1280]{1,0:T(8,128)(2,1)} %param.15, f32[640,64]{1,0:T(8,128)S(1)} %reshape.78, f32[640]{0:T(1024)S(1)} %copy-done.6, f32[64]{0:T(128)S(1)} %add_rsqrt_fusion), kind=kOutput, calls=%fused_computation.10 | convolution fusion | flops 215244800 | bytes 3689216 | tf_op jit(solution)/shard_map/dot_general | solution.py:127
  (15 shorter events, 0.1 us)
Async XLA Ops:
  0.0 64.4 %copy-start = (bf16[1280,640]{1,0:T(8,128)(2,1)S(1)}, bf16[1280,640]{1,0:T(8,128)(2,1)}, u32[]{:S(2)}) copy-start(bf16[1280,640]{1,0:T(8,128)(2,1)} %param.16) | copy-start | bytes 4915204
  0.0 32.4 %copy-start.3 = (f32[4,8,1056]{2,1,0:T(8,128)S(1)}, f32[4,8,1056]{2,1,0:T(8,128)}, u32[]{:S(2)}) copy-start(f32[4,8,1056]{2,1,0:T(8,128)} %constant.134) | copy-start | bytes 405508
  0.0 32.4 %copy-start.2 = (f32[8,8,1056]{2,1,0:T(8,128)S(1)}, f32[8,8,1056]{2,1,0:T(8,128)}, u32[]{:S(2)}) copy-start(f32[8,8,1056]{2,1,0:T(8,128)} %constant.135) | copy-start | bytes 811012
  0.0 6.2 %collective-permute-start = (f32[80,32]{0,1:T(8,128)}, f32[80,32]{0,1:T(8,128)S(1)}, u32[]{:S(2)}, u32[]{:S(2)}) collective-permute-start(f32[80,32]{0,1:T(8,128)} %param.12), channel_id=1, source_target_pairs={{0,1},{1,2},{2,3},{3,4},{4,5},{5,6},{6,7},{7,0},{8,9},{9,10},{10,1... | collective-permute-start | bytes 30728 | tf_op jit(solution)/shard_map/ppermute | solution.py:246
  6.2 5.0 %collective-permute-start.1 = (f32[80,32]{0,1:T(8,128)S(1)}, f32[80,32]{0,1:T(8,128)S(1)}, u32[]{:S(2)}, u32[]{:S(2)}) collective-permute-start(f32[80,32]{0,1:T(8,128)S(1)} %collective-permute-done), channel_id=1, source_target_pairs={{0,1},{1,2},{2,3},{3,4},{4,5},{5,6},{6,7},{7,0},{8,9},{9,10},{10,1... | collective-permute-start | bytes 30728 | tf_op jit(solution)/shard_map/ppermute | solution.py:246
  11.2 5.0 %collective-permute-start.2 = (f32[80,32]{0,1:T(8,128)S(1)}, f32[80,32]{0,1:T(8,128)S(1)}, u32[]{:S(2)}, u32[]{:S(2)}) collective-permute-start(f32[80,32]{0,1:T(8,128)S(1)} %collective-permute-done.1), channel_id=1, source_target_pairs={{0,1},{1,2},{2,3},{3,4},{4,5},{5,6},{6,7},{7,0},{8,9},{9,10},{10,1... | collective-permute-start | bytes 30728 | tf_op jit(solution)/shard_map/ppermute | solution.py:246
  16.1 9.9 %collective-permute-start.3 = (f32[80,32]{0,1:T(8,128)S(1)}, f32[80,32]{0,1:T(8,128)S(1)}, u32[]{:S(2)}, u32[]{:S(2)}) collective-permute-start(f32[80,32]{0,1:T(8,128)S(1)} %collective-permute-done.2), channel_id=1, source_target_pairs={{0,1},{1,2},{2,3},{3,4},{4,5},{5,6},{6,7},{7,0},{8,9},{9,10},{10,1... | collective-permute-start | bytes 30728 | tf_op jit(solution)/shard_map/ppermute | solution.py:246
  19.7 22.2 %all-to-all-start = ((bf16[32,2,640]{2,1,0:T(2,128)(2,1)}), bf16[32,2,640]{2,1,0:T(2,128)(2,1)S(1)}, u32[]{:S(2)}, u32[]{:S(2)}) async-start(bf16[32,2,640]{2,1,0:T(2,128)(2,1)} %reshape.80), calls=%async_computation | async-start | bytes 163840 | tf_op jit(solution)/shard_map/all_to_all | solution.py:238
  26.0 15.7 %copy-start.5 = (f32[80,32]{0,1:T(8,128)S(1)}, f32[80,32]{0,1:T(8,128)}, u32[]{:S(2)}) copy-start(f32[80,32]{0,1:T(8,128)} %param.12) | copy-start | bytes 30724
  26.1 5.8 %collective-permute-start.4 = (f32[80,32]{0,1:T(8,128)S(1)}, f32[80,32]{0,1:T(8,128)S(1)}, u32[]{:S(2)}, u32[]{:S(2)}) collective-permute-start(f32[80,32]{0,1:T(8,128)S(1)} %collective-permute-done.3), channel_id=1, source_target_pairs={{0,1},{1,2},{2,3},{3,4},{4,5},{5,6},{6,7},{7,0},{8,9},{9,10},{10,1... | collective-permute-start | bytes 30728 | tf_op jit(solution)/shard_map/ppermute | solution.py:246
  31.8 5.0 %collective-permute-start.5 = (f32[80,32]{0,1:T(8,128)S(1)}, f32[80,32]{0,1:T(8,128)S(1)}, u32[]{:S(2)}, u32[]{:S(2)}) collective-permute-start(f32[80,32]{0,1:T(8,128)S(1)} %collective-permute-done.4), channel_id=1, source_target_pairs={{0,1},{1,2},{2,3},{3,4},{4,5},{5,6},{6,7},{7,0},{8,9},{9,10},{10,1... | collective-permute-start | bytes 30728 | tf_op jit(solution)/shard_map/ppermute | solution.py:246
  35.9 10.0 %copy-start.4 = (f32[32,1056]{1,0:T(8,128)S(1)}, f32[32,1056]{1,0:T(8,128)}, u32[]{:S(2)}) copy-start(f32[32,1056]{1,0:T(8,128)} %constant.129.clone) | copy-start | bytes 405508
  36.8 5.0 %collective-permute-start.6 = (f32[80,32]{0,1:T(8,128)S(1)}, f32[80,32]{0,1:T(8,128)S(1)}, u32[]{:S(2)}, u32[]{:S(2)}) collective-permute-start(f32[80,32]{0,1:T(8,128)S(1)} %collective-permute-done.5), channel_id=1, source_target_pairs={{0,1},{1,2},{2,3},{3,4},{4,5},{5,6},{6,7},{7,0},{8,9},{9,10},{10,1... | collective-permute-start | bytes 30728 | tf_op jit(solution)/shard_map/ppermute | solution.py:246
  42.6 3.8 %copy-start.1 = (bf16[4,8,8,8,1056]{4,3,2,1,0:T(8,128)(2,1)S(1)}, bf16[4,8,8,8,1056]{4,3,2,1,0:T(8,128)(2,1)}, u32[]{:S(2)}) copy-start(bf16[4,8,8,8,1056]{4,3,2,1,0:T(8,128)(2,1)} %multiply_convert_fusion) | copy-start | bytes 12976132
  49.2 15.2 %copy-start.6 = (f32[640]{0:T(1024)S(1)}, f32[640]{0:T(1024)}, u32[]{:S(2)}) copy-start(f32[640]{0:T(1024)} %param.14) | copy-start | bytes 7684
